TPU v7x, 256 devices: a whole 4x4x8 slice. The times are simulated.
256 devices in a mesh: img: 4 (over y_hi, core), txt: 64 (over x, y_lo, z).
Axes of the slice: x: 4, y: 4 (y_hi: 2, y_lo: 2; y = y_hi * 2 + y_lo), z: 8, core: 2. Of those that a mesh axis runs over, the one named last changes fastest.
Arguments:
- queries: bfloat16 [1, 40960, 8192], P(None, 'txt', 'img'), may hold values from -128 to 128
- visual_keys: bfloat16 [1, 512, 8192], P(None, 'img'), may hold values from -5 to 5
- visual_values: bfloat16 [1, 512, 8192], P(None, 'img'), may hold values from -6 to 6
- out_grad: bfloat16 [1, 40960, 8192], P(None, 'txt', 'img'), may hold values from -6 to 6
- gate_value: float32 [1, 64], P(None, 'img'), may hold values from -1.5 to 1.5
- image_order: int32 [1, 8], replicated, may hold values from 0 to 7, as said below
- image_seen: int32 [40960], P('txt'), may hold values from 1 to 8
Outputs:
- query_grad: bfloat16 [1, 40960, 8192], P(None, 'txt', 'img')
- key_grad: float32 [1, 512, 8192], P(None, 'txt', 'img')
- value_grad: float32 [1, 512, 8192], P(None, 'txt', 'img')
Inputs may be any that keep to these rules, and one draw needn't show every extreme that they name: `image_order`: each row names every image of 0 to 7 once.
All inputs are finite; a program needn't handle non-finite values.
Results may differ from a plain program's by a relative error of at most 0.0058.
Values may be sent and summed in bfloat16 or wider, within the bound.
A program may use at most 128 MiB of HBM per device.

v0:
```python
import math

import jax
import jax.numpy as jnp
from jax import lax
from jax.sharding import PartitionSpec as P


def cut_along(shard, dim, peers):
    before, after = (shard.shape[:dim], shard.shape[dim + 1 :])
    return jnp.moveaxis(shard.reshape(*before, peers, -1, *after), dim, 0)


def summed_on_arrival(shard, axis, dim):
    blocks = cut_along(shard, dim, lax.axis_size(axis))
    arrived = lax.all_to_all(blocks, axis, split_axis=0, concat_axis=0, tiled=True)
    return arrived.astype(jnp.float32).sum(axis=0)


def in_one_piece(arrays, axis, dim, along):
    both = jnp.concatenate(arrays, axis=along)
    result, at, finished = (summed_on_arrival(both, axis, dim), 0, [])
    for a in arrays:
        finished.append(lax.slice_in_dim(result, at, at + a.shape[along], axis=along))
        at += a.shape[along]
    return tuple(finished)


def image_mask(order_row, image_seen, key_count):
    image_count = order_row.shape[0]
    latent_count = key_count // image_count
    key_image = jnp.broadcast_to(order_row[:, None], (image_count, latent_count)).reshape(key_count)
    return key_image[None, :] < image_seen[:, None]


def attention_grads(query, grad_in, factor, key_rows, value_rows, allowed, score_scale):
    token_count = query.shape[0]
    head_count = factor.shape[0]
    head_width = query.shape[1] // head_count
    key_count = key_rows.shape[0]
    query_heads = query.reshape(token_count, head_count, head_width)
    key_heads = key_rows.reshape(key_count, head_count, head_width)
    value_heads = value_rows.reshape(key_count, head_count, head_width)
    gated_grad = (
        grad_in.reshape(token_count, head_count, head_width).astype(jnp.float32)
        * factor[None, :, None]
    ).astype(jnp.bfloat16)
    scores = (
        jnp.einsum("thd,khd->htk", query_heads, key_heads, preferred_element_type=jnp.float32)
        * score_scale
    )
    masked = jnp.where(allowed[None], scores, -1e30)
    row_max = jnp.max(masked, axis=2, keepdims=True)
    exponent = jnp.where(allowed[None], jnp.exp(masked - row_max), 0.0)
    weights = exponent / jnp.sum(exponent, axis=2, keepdims=True)
    weight_half = weights.astype(jnp.bfloat16)
    attended = jnp.einsum(
        "htk,khd->thd", weight_half, value_heads, preferred_element_type=jnp.float32
    )
    row_delta = jnp.sum(gated_grad.astype(jnp.float32) * attended, axis=2)
    weight_grad = jnp.einsum(
        "thd,khd->htk", gated_grad, value_heads, preferred_element_type=jnp.float32
    )
    score_half = (weights * (weight_grad - jnp.transpose(row_delta)[:, :, None])).astype(
        jnp.bfloat16
    )
    query_part = (
        jnp.einsum("htk,khd->thd", score_half, key_heads, preferred_element_type=jnp.float32)
        * score_scale
    )
    return (
        query_part.astype(jnp.bfloat16).reshape(token_count, -1),
        score_half,
        weight_half,
        query_heads,
        gated_grad,
    )


def latent_terms(score_half, weight_half, query_heads, gated_grad, count, score_scale):
    key_part = (
        jnp.einsum("htk,thd->khd", score_half, query_heads, preferred_element_type=jnp.float32)
        * score_scale
    )
    value_part = jnp.einsum(
        "htk,thd->khd", weight_half, gated_grad, preferred_element_type=jnp.float32
    )
    return (key_part.reshape(count, -1), value_part.reshape(count, -1))


def shards(queries, visual_keys, visual_values, out_grad, gate_value, image_order, image_seen):
    width_local = queries.shape[2]
    head_width = width_local // gate_value.shape[1]
    score_scale = 1.0 / math.sqrt(head_width)
    key_rows = lax.all_to_all(visual_keys[0], "img", split_axis=1, concat_axis=0, tiled=True)
    value_rows = lax.all_to_all(visual_values[0], "img", split_axis=1, concat_axis=0, tiled=True)
    key_total = key_rows.shape[0]
    allowed = image_mask(image_order[0], image_seen, key_total)
    factor = jnp.tanh(gate_value[0])
    query_part, score_half, weight_half, query_heads, gated_grad = attention_grads(
        queries[0], out_grad[0], factor, key_rows, value_rows, allowed, score_scale
    )
    query_list = [query_part]
    key_part, value_part = latent_terms(
        score_half, weight_half, query_heads, gated_grad, key_total, score_scale
    )
    key_share, value_share = in_one_piece(
        (key_part.astype(jnp.bfloat16), value_part.astype(jnp.bfloat16)), "txt", 0, 1
    )
    key_list = [key_share]
    value_list = [value_share]
    key_grad = jnp.stack(key_list)
    value_grad = jnp.stack(value_list)
    return (jnp.stack(query_list), key_grad, value_grad)


def solution(mesh):
    placed = (
        P(None, "txt", "img"),
        P(None, "img", None),
        P(None, "img", None),
        P(None, "txt", "img"),
        P(None, "img"),
        P(),
        P("txt"),
    )
    return jax.shard_map(
        shards,
        mesh=mesh,
        in_specs=placed,
        out_specs=(P(None, "txt", "img"), P(None, "txt", "img"), P(None, "txt", "img")),
        check_vma=False,
    )
```

profile of v0, /device:TPU:2, one launch (start us, length us, event | category | flops | bytes accessed | tf_op | source)
XLA Modules:
  0.0 285.8 jit_solution(16032215586573750900)
XLA Ops:
  0.6 3.3 %all_to_all.27 = bf16[128,4,2048]{2,1,0:T(4,128)(2,1)S(1)} reshape(bf16[1,128,8192]{2,1,0:T(8,128)(2,1)} %param.8) | data formatting | bytes 4194304 | tf_op jit(solution)/shard_map/all_to_all | solution.py:95
  4.0 2.5 copy.21
  6.4 4.5 %all-to-all-start = ((bf16[128,4,2048]{2,0,1:T(8,128)(2,1)}), bf16[128,4,2048]{2,0,1:T(8,128)(2,1)S(1)}, u32[]{:S(2)}, u32[]{:S(2)}) async-start(bf16[128,4,2048]{2,0,1:T(8,128)(2,1)} %copy.21), calls=%async_computation | async-start | bytes 4194304 | tf_op jit(solution)/shard_map/all_to_all | solution.py:95
  10.9 4.5 %all_to_all.30 = bf16[128,4,2048]{2,1,0:T(4,128)(2,1)} reshape(bf16[1,128,8192]{2,1,0:T(8,128)(2,1)} %param.9) | data formatting | bytes 4194304 | tf_op jit(solution)/shard_map/all_to_all | solution.py:96
  15.4 4.1 %copy.25 = bf16[128,4,2048]{2,0,1:T(8,128)(2,1)} copy(bf16[128,4,2048]{2,1,0:T(4,128)(2,1)} %all_to_all.30) | data formatting | bytes 4194304 | tf_op jit(solution)/shard_map/all_to_all | solution.py:96
  19.5 0.0 copy-start.2
  19.5 18.6 %all-to-all-done = bf16[128,4,2048]{2,0,1:T(8,128)(2,1)S(1)} async-done(((bf16[128,4,2048]{2,0,1:T(8,128)(2,1)}), bf16[128,4,2048]{2,0,1:T(8,128)(2,1)S(1)}, u32[]{:S(2)}, u32[]{:S(2)}) %all-to-all-start) | async-done | bytes 2097184 | tf_op jit(solution)/shard_map/all_to_all | solution.py:95
  38.1 4.6 %all-to-all-start.1 = ((bf16[128,4,2048]{2,0,1:T(8,128)(2,1)}), bf16[128,4,2048]{2,0,1:T(8,128)(2,1)}, u32[]{:S(2)}, u32[]{:S(2)}) async-start(bf16[128,4,2048]{2,0,1:T(8,128)(2,1)} %copy.25), calls=%async_computation.1 | async-start | bytes 4194304 | tf_op jit(solution)/shard_map/all_to_all | solution.py:96
  42.7 4.1 %copy.44 = bf16[80,8,16,128]{3,2,1,0:T(8,128)(2,1)} copy(bf16[80,8,16,128]{3,1,2,0:T(8,128)(2,1)} %bitcast.48) | data formatting | bytes 5242880
  46.8 0.0 copy-start.3
  46.8 0.0 copy-start.1
  46.8 0.0 copy-done.2
  46.8 0.1 broadcast_in_dim.33
  46.9 0.1 lt.19
  47.0 4.9 %copy.24 = f32[1,640,2048]{1,2,0:T(8,128)} copy(bf16[1,640,2048]{2,1,0:T(8,128)(2,1)} %param.10) | data formatting | bytes 7864320 | tf_op jit(solution)/shard_map/convert_element_type | solution.py:45
  51.9 0.0 copy-done.3
  51.9 0.0 copy-done.1
  51.9 0.3 broadcast_compare_fusion
  52.1 4.6 %multiply_convert_fusion.2 = bf16[640,16,128]{0,2,1:T(8,128)(2,1)} fusion(f32[640,16,128]{0,2,1:T(8,128)} %bitcast.41, f32[16]{0:T(128)S(1)} %tanh_bitcast_fusion), kind=kLoop, calls=%fused_computation.14 | loop fusion | flops 2621440 | bytes 7864384 | tf_op jit(solution)/shard_map/convert_element_type | solution.py:47
  56.7 2.0 copy.43
  58.7 3.0 %copy.32 = bf16[512,16,128]{0,2,1:T(8,128)(2,1)S(1)} copy(bf16[512,16,128]{2,1,0:T(8,128)(2,1)} %bitcast.46) | data formatting | bytes 4194304 | tf_op jit(solution)/shard_map/reshape | solution.py:42
  61.7 8.1 %all-to-all-done.1 = bf16[128,4,2048]{2,0,1:T(8,128)(2,1)} async-done(((bf16[128,4,2048]{2,0,1:T(8,128)(2,1)}), bf16[128,4,2048]{2,0,1:T(8,128)(2,1)}, u32[]{:S(2)}, u32[]{:S(2)}) %all-to-all-start.1) | async-done | bytes 2097184 | tf_op jit(solution)/shard_map/all_to_all | solution.py:96
  69.8 3.6 %copy.45 = bf16[64,8,16,128]{3,2,1,0:T(8,128)(2,1)} copy(bf16[64,8,16,128]{3,1,2,0:T(8,128)(2,1)} %bitcast.21) | data formatting | bytes 4194304
  73.3 4.3 %copy.29 = bf16[512,16,128]{0,2,1:T(8,128)(2,1)} copy(bf16[512,16,128]{2,1,0:T(8,128)(2,1)} %bitcast.47) | data formatting | bytes 4194304 | tf_op jit(solution)/shard_map/reshape | solution.py:43
  77.7 11.0 %fusion.9 = f32[16,640,512]{1,2,0:T(8,128)} fusion(bf16[512,16,128]{0,2,1:T(8,128)(2,1)S(1)} %copy.32, bf16[640,16,128]{2,1,0:T(8,128)(2,1)} %bitcast.43), kind=kOutput, calls=%fused_computation.19 | convolution fusion | flops 1342177280 | bytes 25690112 | tf_op jit(solution)/shard_map/thd,khd->htk/dot_general | solution.py:49
  88.7 25.2 %fusion.16 = (f32[16,640]{1,0:T(8,128)S(1)}, f32[16,640,512]{1,2,0:T(8,128)}) fusion(f32[16,640,512]{1,2,0:T(8,128)} %fusion.9, pred[640,512]{0,1:T(8,128)(4,1)S(1)} %broadcast_compare_fusion), kind=kOutput, calls=%fused_computation.29 | output fusion | flops 36700672 | bytes 42311680 | tf_op jit(solution)/shard_map/sub | solution.py:54
  113.9 8.5 %fusion.5 = bf16[16,640,512]{1,2,0:T(8,128)(2,1)S(1)} fusion(f32[16,640,512]{1,2,0:T(8,128)} %get-tuple-element.12, f32[16,640]{1,0:T(8,128)S(1)} %get-tuple-element.11), kind=kLoop, calls=%fused_computation.9 | loop fusion | flops 10485760 | bytes 31498240 | tf_op jit(solution)/shard_map/convert_element_type | solution.py:56
  122.4 6.4 %convert_bitcast_fusion = bf16[512,16,128]{0,2,1:T(8,128)(2,1)} fusion(bf16[640,16,128]{0,2,1:T(8,128)(2,1)} %multiply_convert_fusion.2, bf16[16,640,512]{1,2,0:T(8,128)(2,1)S(1)} %fusion.5), kind=kOutput, calls=%fused_computation.22 | convolution fusion | flops 1343225856 | bytes 15204352 | tf_op jit(solution)/shard_map/htk,thd->khd/dot_general | solution.py:85
  128.9 4.2 %fusion.6 = f32[640,16]{0,1:T(8,128)S(1)} fusion(bf16[640,16,128]{0,2,1:T(8,128)(2,1)} %multiply_convert_fusion.2, bf16[512,16,128]{0,2,1:T(8,128)(2,1)} %copy.29, bf16[16,640,512]{1,2,0:T(8,128)(2,1)S(1)} %fusion.5), kind=kOutput, calls=%fused_computation.12 | convolution fusion | flops 1346099200 | bytes 15245312 | tf_op jit(solution)/shard_map/htk,khd->thd/dot_general | solution.py:57
  133.1 0.0 copy-start
  133.1 14.2 %multiply_convert_fusion = bf16[16,640,512]{1,2,0:T(8,128)(2,1)} fusion(f32[16,640]{1,0:T(8,128)S(1)} %bitcast.49, f32[16,640,512]{1,2,0:T(8,128)} %get-tuple-element.12, f32[16,640]{1,0:T(8,128)S(1)} %get-tuple-element.11, bf16[512,16,128]{0,2,1:T(8,128)(2,1)} %copy.29, bf16[640,16,128]{0,2,1:T(8,128)(2,1)} %multiply_convert_fusion.2), kind=kOutput, calls=%fused_computation.1 | convolution fusion | flops 1363148800 | bytes 36257792 | tf_op jit(solution)/shard_map/thd,khd->htk/dot_general | solution.py:61
  147.3 0.0 copy-done
  147.3 7.0 %fusion.11 = bf16[512,16,128]{2,0,1:T(8,128)(2,1)S(1)} fusion(bf16[16,640,512]{1,2,0:T(8,128)(2,1)} %multiply_convert_fusion, bf16[640,16,128]{2,1,0:T(8,128)(2,1)S(1)} %bitcast.44), kind=kOutput, calls=%fused_computation.21 | convolution fusion | flops 1344274432 | bytes 15204352 | tf_op jit(solution)/shard_map/htk,thd->khd/dot_general | solution.py:82
  154.3 2.7 copy.34
  156.9 4.2 %convert_element_type.57 = bf16[64,8,2048]{2,1,0:T(8,128)(2,1)} reshape(bf16[512,16,128]{2,1,0:T(8,128)(2,1)} %copy.34) | data formatting | bytes 4194304 | tf_op jit(solution)/shard_map/convert_element_type | solution.py:108
  161.1 4.5 %copy.36 = bf16[512,16,128]{2,1,0:T(8,128)(2,1)} copy(bf16[512,16,128]{0,2,1:T(8,128)(2,1)} %convert_bitcast_fusion) | data formatting | bytes 4194304 | tf_op jit(solution)/shard_map/convert_element_type | solution.py:108
  165.6 4.2 %convert_element_type.60 = bf16[64,8,2048]{2,1,0:T(8,128)(2,1)} reshape(bf16[512,16,128]{2,1,0:T(8,128)(2,1)} %copy.36) | data formatting | bytes 4194304 | tf_op jit(solution)/shard_map/convert_element_type | solution.py:108
  169.8 4.7 %pad_maximum_fusion = bf16[64,8,4096]{2,1,0:T(8,128)(2,1)} fusion(bf16[64,8,2048]{2,1,0:T(8,128)(2,1)} %convert_element_type.60, bf16[64,8,2048]{2,1,0:T(8,128)(2,1)} %convert_element_type.57), kind=kLoop, calls=%fused_computation.15 | loop fusion | flops 8388608 | bytes 8388608 | tf_op jit(solution)/shard_map/concatenate | solution.py:21
  174.4 12.3 %all-to-all-start.2 = ((bf16[64,8,4096]{2,1,0:T(8,128)(2,1)}), bf16[64,8,4096]{2,1,0:T(8,128)(2,1)}, u32[]{:S(2)}, u32[]{:S(2)}) async-start(bf16[64,8,4096]{2,1,0:T(8,128)(2,1)} %pad_maximum_fusion), calls=%async_computation.2 | async-start | bytes 8388608 | tf_op jit(solution)/shard_map/all_to_all | solution.py:16
  186.8 7.4 %multiply_convert_fusion.1 = bf16[16,640,128]{1,2,0:T(8,128)(2,1)} fusion(bf16[512,16,128]{0,2,1:T(8,128)(2,1)S(1)} %copy.32, bf16[16,640,512]{1,2,0:T(8,128)(2,1)} %multiply_convert_fusion), kind=kOutput, calls=%fused_computation.13 | convolution fusion | flops 1344798720 | bytes 15204352 | tf_op jit(solution)/shard_map/htk,khd->thd/dot_general | solution.py:68
  194.2 4.4 %copy.37 = bf16[1,640,2048]{2,1,0:T(8,128)(2,1)} copy(bf16[1,640,2048]{1,2,0:T(8,128)(2,1)} %bitcast.42) | data formatting | bytes 5242880
  198.6 83.8 %all-to-all-done.2 = bf16[64,8,4096]{2,1,0:T(8,128)(2,1)} async-done(((bf16[64,8,4096]{2,1,0:T(8,128)(2,1)}), bf16[64,8,4096]{2,1,0:T(8,128)(2,1)}, u32[]{:S(2)}, u32[]{:S(2)}) %all-to-all-start.2) | async-done | bytes 4194336 | tf_op jit(solution)/shard_map/all_to_all | solution.py:16
  282.4 2.8 convert_reduce_fusion
  285.2 0.7 slice_bitcast_fusion
  (1 shorter events, 0.0 us)
Async XLA Ops:
  6.4 31.6 %all-to-all-start = ((bf16[128,4,2048]{2,0,1:T(8,128)(2,1)}), bf16[128,4,2048]{2,0,1:T(8,128)(2,1)S(1)}, u32[]{:S(2)}, u32[]{:S(2)}) async-start(bf16[128,4,2048]{2,0,1:T(8,128)(2,1)} %copy.21), calls=%async_computation | async-start | bytes 4194304 | tf_op jit(solution)/shard_map/all_to_all | solution.py:95
  19.5 27.3 %copy-start.2 = (s32[1,8]{1,0:T(1,128)S(1)}, s32[1,8]{1,0:T(1,128)}, u32[]{:S(2)}) copy-start(s32[1,8]{1,0:T(1,128)} %param.12) | copy-start | bytes 100
  38.1 31.7 %all-to-all-start.1 = ((bf16[128,4,2048]{2,0,1:T(8,128)(2,1)}), bf16[128,4,2048]{2,0,1:T(8,128)(2,1)}, u32[]{:S(2)}, u32[]{:S(2)}) async-start(bf16[128,4,2048]{2,0,1:T(8,128)(2,1)} %copy.25), calls=%async_computation.1 | async-start | bytes 4194304 | tf_op jit(solution)/shard_map/all_to_all | solution.py:96
  46.8 5.1 %copy-start.3 = (f32[1,16]{1,0:T(1,128)S(1)}, f32[1,16]{1,0:T(1,128)}, u32[]{:S(2)}) copy-start(f32[1,16]{1,0:T(1,128)} %param.11) | copy-start | bytes 196
  46.8 5.1 %copy-start.1 = (s32[640]{0:T(1024)S(1)}, s32[640]{0:T(1024)}, u32[]{:S(2)}) copy-start(s32[640]{0:T(1024)} %param.13) | copy-start | bytes 7684
  133.1 14.2 %copy-start = (bf16[80,8,16,128]{3,2,1,0:T(8,128)(2,1)S(1)}, bf16[80,8,16,128]{3,2,1,0:T(8,128)(2,1)}, u32[]{:S(2)}) copy-start(bf16[80,8,16,128]{3,2,1,0:T(8,128)(2,1)} %copy.44) | copy-start | bytes 7864324
  174.4 107.9 %all-to-all-start.2 = ((bf16[64,8,4096]{2,1,0:T(8,128)(2,1)}), bf16[64,8,4096]{2,1,0:T(8,128)(2,1)}, u32[]{:S(2)}, u32[]{:S(2)}) async-start(bf16[64,8,4096]{2,1,0:T(8,128)(2,1)} %pad_maximum_fusion), calls=%async_computation.2 | async-start | bytes 8388608 | tf_op jit(solution)/shard_map/all_to_all | solution.py:16
where the time goes:
time: 287 us; the launch traced here: 286 us
  waiting for transfers between devices  110 us (38%)
  local copies, waits for them, and re-layouts  57 us (20%)
  matrix products  50.2 us (17%)
  other arithmetic  46 us (16%)
  starting transfers between devices  21.4 us (7%)
    all_to_all x1, waiting for transfers between devices, summed_on_arrival(): lax.all_to_all(blocks, axis, split_axis=0, concat_axis=0, tiled=True)  83.8 us
    sub x1, other arithmetic, attention_grads(): exponent = jnp.where(allowed[None], jnp.exp(masked - row_max), 0.0)  25.2 us
    all_to_all x1, waiting for transfers between devices, shards(): lax.all_to_all(visual_keys[0], 'img', split_axis=1, concat_axis=0, tiled=...  18.6 us
    dot_general x1, matrix products, attention_grads(): jnp.einsum('thd,khd->htk', gated_grad, value_heads, preferred_element_typ...  14.2 us
    unnamed x12, local copies, waits for them, and re-layouts  14 us
    all_to_all x1, starting transfers between devices, summed_on_arrival(): lax.all_to_all(blocks, axis, split_axis=0, concat_axis=0, tiled=True)  12.3 us
    dot_general x1, matrix products, attention_grads(): jnp.einsum('thd,khd->htk', query_heads, key_heads, preferred_element_type...  11 us
    convert_element_type x2, local copies, waits for them, and re-layouts, shards(): value_part.astype(jnp.bfloat16)  8.68 us
  transfers between devices with their start and end apart: 3, of which 3 were waited for; matrix products, arithmetic and copies ran while one was open for 12% of the time, Pallas kernels for 0%

commit v1 on v0

v1 whole, which is shorter than its diff:
```python
import functools
import math

import jax
import jax.numpy as jnp
from jax import lax
from jax.experimental import pallas as pl
from jax.experimental.pallas import tpu as pltpu
from jax.sharding import PartitionSpec as P

MESH = pl.DeviceIdType.MESH
F32, BF16 = jnp.float32, jnp.bfloat16
HEAD = 128
LATENTS = 64
NX, NLO, NZ = 4, 2, 8
GROUP = NLO * NZ


def product(a, b, ca, cb):
    return lax.dot_general(a, b, (((ca,), (cb,)), ((), ())), preferred_element_type=F32)


def kernel(
    chunks, per, q_hbm, k_hbm, v_hbm, g_hbm, gate, order, seen, dq_hbm, kg_ref, vg_ref,
    q_s, g_s, kv_s, dq_s, may_s, part_s, a_s, b_s, bc_s, zs_s, rz_s,
    own_sem, cross_tx, cross_rx, mate_tx, mate_rx, relay_tx, relay_rx,
    first_tx, a_rx, b_tx, bc_rx, z_tx, z_rx, dq_sem,
):
    img, txt = lax.axis_index("img"), lax.axis_index("txt")
    hi, core = img // 2, lax.rem(img, 2)
    x, lo, z = txt // GROUP, lax.rem(txt // NZ, NLO), lax.rem(txt, NZ)
    slot = lax.rem(txt, GROUP)
    tokens, width = q_s.shape
    block = k_hbm.shape[1]
    half = block // 2
    keys = 4 * block
    images = keys // LATENTS
    cw = per * HEAD
    slab = keys // NX
    scale = 1.0 / math.sqrt(HEAD)
    scale2 = scale * math.log2(math.e)

    mate = (hi * 2 + 1 - core, txt)
    flipped = txt + (1 - 2 * lo) * NZ
    cross = [((1 - hi) * 2 + c, flipped) for c in range(2)]
    relay = (img, flipped)
    xp, xm, xo = lax.rem(x + 1, NX), lax.rem(x + NX - 1, NX), lax.rem(x + 2, NX)
    up, down = (img, xp * GROUP + slot), (img, xm * GROUP + slot)

    def in_group(j):
        other = lax.rem(slot + j, GROUP)
        return other, (img, x * GROUP + other)

    def local(src, dst, sem):
        return pltpu.make_async_copy(src, dst, sem)

    def remote(src, dst, tx, rx, to):
        return pltpu.make_async_remote_copy(
            src_ref=src, dst_ref=dst, send_sem=tx, recv_sem=rx, device_id=to, device_id_type=MESH
        )

    def columns(c, base=0):
        return pl.ds(pl.multiple_of(base + c * cw, HEAD), cw)

    def rows(start, size):
        return pl.ds(pl.multiple_of(start, 16), size)

    own_columns = pl.ds(pl.multiple_of(img * width, HEAD), width)
    loads = [
        local(k_hbm.at[0, :, own_columns], kv_s.at[0, img], own_sem.at[0]),
        local(v_hbm.at[0, :, own_columns], kv_s.at[1, img], own_sem.at[1]),
        local(q_hbm.at[0], q_s, own_sem.at[2]),
        local(g_hbm.at[0], g_s, own_sem.at[3]),
    ]
    for copy in loads:
        copy.start()

    barrier = pltpu.get_barrier_semaphore()
    for to in [mate, *cross, up, down]:
        pl.semaphore_signal(barrier, inc=1, device_id=to, device_id_type=MESH)

    def greet(j, carry):
        pl.semaphore_signal(barrier, inc=1, device_id=in_group(j)[1], device_id_type=MESH)
        return carry

    lax.fori_loop(1, GROUP, greet, 0)
    pl.semaphore_wait(barrier, 5 + GROUP - 1)

    def cross_piece(c):
        return kv_s.at[:, pl.ds(2 * (1 - hi), 2), rows(lo * half, half), columns(c)]

    def relay_piece(c):
        return kv_s.at[:, pl.ds(2 * (1 - hi), 2), rows((1 - lo) * half, half), columns(c)]

    def mate_piece(c):
        return kv_s.at[:, hi * 2 + 1 - core, :, columns(c)]

    def send_latents(c, carry):
        for to in cross:
            for a, src in enumerate((k_hbm, v_hbm)):
                remote(
                    src.at[0, rows((1 - lo) * half, half), columns(c, to[0] * width)],
                    kv_s.at[a, img, rows((1 - lo) * half, half), columns(c)],
                    cross_tx.at[c], cross_rx.at[c], to,
                ).start()
        for a, src in enumerate((k_hbm, v_hbm)):
            remote(
                src.at[0, :, columns(c, mate[0] * width)],
                kv_s.at[a, img, :, columns(c)],
                mate_tx.at[c], mate_rx.at[c], mate,
            ).start()
        return carry

    lax.fori_loop(0, chunks, send_latents, 0)

    may_s[...] = jnp.concatenate(
        [jnp.where(order[0, b] < seen[...], 1.0, 0.0) for b in range(images)], axis=0
    )

    def pass_on(c):
        piece = cross_piece(c)
        remote(piece, piece, cross_tx.at[c], cross_rx.at[c], relay).wait_recv()
        remote(piece, piece, relay_tx.at[c], relay_rx.at[c], relay).start()

    def latents_ready(c):
        piece = mate_piece(c)
        remote(piece, piece, mate_tx.at[c], mate_rx.at[c], mate).wait_recv()
        piece = relay_piece(c)
        remote(piece, piece, relay_tx.at[c], relay_rx.at[c], relay).wait_recv()

    def head(c, j):
        h = c * per + j
        cols = pl.ds(pl.multiple_of(h * HEAD, HEAD), HEAD)
        k = kv_s[0, :, :, cols].reshape(keys, HEAD)
        v = kv_s[1, :, :, cols].reshape(keys, HEAD)
        q = q_s[:, cols]
        factor = jnp.tanh(jnp.full((8, HEAD), gate[0, h], F32))[0:1]
        gated = (g_s[:, cols].astype(F32) * factor).astype(BF16)
        may = may_s[...] > 0
        scores = product(k, q, 1, 1).reshape(images, LATENTS, tokens)
        top = jnp.where(may, jnp.max(scores, axis=1), -1e30)
        top = jnp.max(top, axis=0, keepdims=True)
        off = jnp.where(may, top, 1e30)
        exponent = jnp.exp2((scores - off[:, None, :]) * scale2).reshape(keys, tokens)
        weights = exponent * (1.0 / jnp.sum(exponent, axis=0, keepdims=True))
        weight_grad = product(v, gated, 1, 1)
        delta = jnp.sum(weights * weight_grad, axis=0, keepdims=True)
        score_half = (weights * (weight_grad - delta)).astype(BF16)
        weight_half = weights.astype(BF16)
        at = pl.ds(j * HEAD, HEAD)
        value_part = product(weight_half, gated, 1, 0)
        part_s[c, 1, :, :, at] = value_part.astype(BF16).reshape(NX, slab, HEAD)
        key_part = product(score_half, q, 1, 0) * scale
        part_s[c, 0, :, :, at] = key_part.astype(BF16).reshape(NX, slab, HEAD)
        dq_s[:, cols] = (product(score_half, k, 0, 0) * scale).astype(BF16)

    def dq_copy(c):
        return local(dq_s.at[:, columns(c)], dq_hbm.at[0, :, columns(c)], dq_sem.at[c])

    def first_sends(c):
        return [
            remote(part_s.at[c, 0, xo], a_s.at[c, 0], first_tx.at[c], a_rx.at[c], down),
            remote(part_s.at[c, 1, xo], a_s.at[c, 1], first_tx.at[c], a_rx.at[c], up),
            remote(part_s.at[c, 0, xp], bc_s.at[c, 1, 0], first_tx.at[c], bc_rx.at[c], up),
            remote(part_s.at[c, 1, xm], bc_s.at[c, 1, 1], first_tx.at[c], bc_rx.at[c], down),
        ]

    def second_sends(c):
        return [
            remote(b_s.at[c, 0], bc_s.at[c, 0, 0], b_tx.at[c], bc_rx.at[c], down),
            remote(b_s.at[c, 1], bc_s.at[c, 0, 1], b_tx.at[c], bc_rx.at[c], up),
        ]

    def second_hop(c):
        piece = a_s.at[c]
        remote(piece, piece, first_tx.at[c], a_rx.at[c], down).wait_recv()
        b_s[c, 0] = (a_s[c, 0].astype(F32) + part_s[c, 0, xm].astype(F32)).astype(BF16)
        b_s[c, 1] = (a_s[c, 1].astype(F32) + part_s[c, 1, xp].astype(F32)).astype(BF16)

    def x_sum(c):
        piece = bc_s.at[c]
        remote(piece, piece, b_tx.at[c], bc_rx.at[c], down).wait_recv()
        both = [
            (
                part_s[c, a, x].astype(F32) + bc_s[c, 0, a].astype(F32) + bc_s[c, 1, a].astype(F32)
            ).reshape(GROUP, slab // GROUP, cw)
            for a in range(2)
        ]
        zs_s[c] = jnp.concatenate(both, axis=1).astype(BF16)
        rz_s[c, slot] = zs_s[c, slot]

    def spread(c):
        def one(j, carry):
            other, to = in_group(j)
            remote(zs_s.at[c, other], rz_s.at[c, slot], z_tx.at[c], z_rx.at[c], to).start()
            return carry

        lax.fori_loop(1, GROUP, one, 0)

    def others(ref):
        return ref.at[pl.ds(0, GROUP - 1)]

    def finish(c):
        piece = others(rz_s.at[c])
        remote(piece, piece, z_tx.at[c], z_rx.at[c], relay).wait_recv()
        total = jnp.sum(rz_s[c].astype(F32), axis=0)
        mine = slab // GROUP
        kg_ref[0, :, columns(c)] = total[:mine]
        vg_ref[0, :, columns(c)] = total[mine:]

    pass_on(0)
    for copy in loads:
        copy.wait()

    def step(s, carry):
        @pl.when(s + 1 < chunks)
        def _():
            pass_on(s + 1)

        @pl.when(s < chunks)
        def _():
            latents_ready(s)

            def one(j, inner):
                head(s, j)
                return inner

            lax.fori_loop(0, per, one, 0)
            dq_copy(s).start()
            for copy in first_sends(s):
                copy.start()

        @pl.when((s >= 1) & (s < chunks + 1))
        def _():
            second_hop(s - 1)
            for copy in second_sends(s - 1):
                copy.start()

        @pl.when((s >= 2) & (s < chunks + 2))
        def _():
            x_sum(s - 2)
            spread(s - 2)

        @pl.when(s >= 3)
        def _():
            finish(s - 3)

        return carry

    lax.fori_loop(0, chunks + 3, step, 0)

    def settle(c, carry):
        dq_copy(c).wait()
        piece = cross_piece(c)
        remote(piece, piece, cross_tx.at[c], cross_rx.at[c], relay).wait_send()
        remote(piece, piece, relay_tx.at[c], relay_rx.at[c], relay).wait_send()
        piece = mate_piece(c)
        remote(piece, piece, mate_tx.at[c], mate_rx.at[c], mate).wait_send()
        piece = bc_s.at[c]
        remote(piece, piece, first_tx.at[c], bc_rx.at[c], down).wait_send()
        piece = b_s.at[c]
        remote(piece, piece, b_tx.at[c], bc_rx.at[c], down).wait_send()
        piece = others(zs_s.at[c])
        remote(piece, piece, z_tx.at[c], z_rx.at[c], relay).wait_send()
        return carry

    lax.fori_loop(0, chunks, settle, 0)


def shards(queries, visual_keys, visual_values, out_grad, gate_value, image_order, image_seen):
    _, tokens, width = queries.shape
    block = visual_keys.shape[1]
    keys = 4 * block
    heads = width // HEAD
    per = 2
    chunks = heads // per
    cw = per * HEAD
    slab = keys // NX
    mine = slab // GROUP
    hbm = pl.BlockSpec(memory_space=pl.ANY)
    vmem = pl.BlockSpec(memory_space=pltpu.VMEM)
    smem = pl.BlockSpec(memory_space=pltpu.SMEM)
    dma = pltpu.SemaphoreType.DMA
    return tuple(
        pl.pallas_call(
            functools.partial(kernel, chunks, per),
            out_shape=(
                jax.ShapeDtypeStruct((1, tokens, width), BF16),
                jax.ShapeDtypeStruct((1, mine, width), F32),
                jax.ShapeDtypeStruct((1, mine, width), F32),
            ),
            in_specs=[hbm, hbm, hbm, hbm, smem, smem, vmem],
            out_specs=(hbm, vmem, vmem),
            scratch_shapes=[
                pltpu.VMEM((tokens, width), BF16),
                pltpu.VMEM((tokens, width), BF16),
                pltpu.VMEM((2, 4, block, width), BF16),
                pltpu.VMEM((tokens, width), BF16),
                pltpu.VMEM((keys // LATENTS, tokens), F32),
                pltpu.VMEM((chunks, 2, NX, slab, cw), BF16),
                pltpu.VMEM((chunks, 2, slab, cw), BF16),
                pltpu.VMEM((chunks, 2, slab, cw), BF16),
                pltpu.VMEM((chunks, 2, 2, slab, cw), BF16),
                pltpu.VMEM((chunks, GROUP, 2 * mine, cw), BF16),
                pltpu.VMEM((chunks, GROUP, 2 * mine, cw), BF16),
                dma((4,)),
            ]
            + [dma((chunks,))] * 13,
            compiler_params=pltpu.CompilerParams(
                collective_id=0, has_side_effects=True, vmem_limit_bytes=60 * 2**20
            ),
            name="attention_grads",
        )(
            queries, visual_keys, visual_values, out_grad, gate_value, image_order,
            image_seen.reshape(1, tokens),
        )
    )


def solution(mesh):
    placed = (
        P(None, "txt", "img"),
        P(None, "img", None),
        P(None, "img", None),
        P(None, "txt", "img"),
        P(None, "img"),
        P(),
        P("txt"),
    )
    return jax.shard_map(
        shards,
        mesh=mesh,
        in_specs=placed,
        out_specs=(P(None, "txt", "img"), P(None, "txt", "img"), P(None, "txt", "img")),
        check_vma=False,
    )
```

time: 287 us -> 79.7 us (0.28)
  waiting for transfers between devices: 110 us -> 0 us
  Pallas kernels: 0 us -> 72.7 us
  local copies, waits for them, and re-layouts: 57 us -> 6.13 us
  matrix products: 50.2 us -> 0 us
  other arithmetic: 46 us -> 0 us
  starting transfers between devices: 21.4 us -> 0 us
    all_to_all x3 -> x0, waiting for transfers between devices: 110 us -> none  [the longest x1 83.8 us: summed_on_arrival(): lax.all_to_all(blocks, axis, split_axis=0, concat_axis=0, tiled=True)]
    pallas_call x0 -> x1, Pallas kernels: none -> 72.7 us  [shards(): pl.pallas_call(functools.partial(kernel, chunks, per), out_shape=(jax.Sha...]
    dot_general x6 -> x0, matrix products: 50.2 us -> none  [the longest x1 14.2 us: attention_grads(): jnp.einsum('thd,khd->htk', gated_grad, value_heads, preferred_element_typ...]
    sub x1 -> x0, other arithmetic: 25.2 us -> none  [attention_grads(): exponent = jnp.where(allowed[None], jnp.exp(masked - row_max), 0.0)]
    all_to_all x3 -> x0, starting transfers between devices: 21.4 us -> none  [the longest x1 12.3 us: summed_on_arrival(): lax.all_to_all(blocks, axis, split_axis=0, concat_axis=0, tiled=True)]
    convert_element_type x5 -> x0, local copies, waits for them, and re-layouts: 20.4 us -> none  [the longest x2 8.68 us: shards(): value_part.astype(jnp.bfloat16)]
    all_to_all x4 -> x0, local copies, waits for them, and re-layouts: 14.4 us -> none  [the longest x2 8.61 us: shards(): lax.all_to_all(visual_values[0], 'img', split_axis=1, concat_axis=0, tile...]
    convert_element_type x2 -> x0, other arithmetic: 13.1 us -> none  [the longest x1 8.53 us: attention_grads(): weight_half = weights.astype(jnp.bfloat16)]
  transfers between devices with their start and end apart: 3 -> 0, of which waited for: 3 -> 0; matrix products, arithmetic and copies ran while one was open for 12% -> 0% of each run, Pallas kernels for 0% -> 0%
where the time goes in v1:
time: 79.7 us; the launch traced here: 79.5 us
  Pallas kernels  72.7 us (91%)
  local copies, waits for them, and re-layouts  6.13 us (8%)
    pallas_call x1, Pallas kernels, shards(): pl.pallas_call(functools.partial(kernel, chunks, per), out_shape=(jax.Sha...  72.7 us
    unnamed x7, local copies, waits for them, and re-layouts  4.86 us

profile of v1, /device:TPU:2, one launch (start us, length us, event | category | flops | bytes accessed | tf_op | source)
XLA Modules:
  0.0 79.5 jit_solution(9190398168358557917)
XLA Ops:
  0.6 1.3 %reshape.9.seen = s32[1,640]{1,0:T(1,128)} reshape(s32[640]{0:T(1024)} %param.13) | data formatting | bytes 5120 | tf_op jit(solution)/shard_map/reshape | solution.py:315
  1.9 72.7 %attention_grads.1 = (bf16[1,640,2048]{2,1,0:T(8,128)(2,1)}, f32[1,8,2048]{2,1,0:T(8,128)}, f32[1,8,2048]{2,1,0:T(8,128)}) custom-call(bf16[1,640,2048]{2,1,0:T(8,128)(2,1)} %q_hbm.1, bf16[1,128,8192]{2,1,0:T(8,128)(2,1)} %k_hbm.1, bf16[1,128,8192]{2,1,0:T(8,128)(2,1)} %v_hbm.1, bf16[1,640,2048]{2,1,0:T(8,128)(2,1)} %g_hbm.1, f32[1,16]{1,0:T(1,128)} %gate.1, ...), custom_call_target="tpu_custom_call" | custom-call | tf_op jit(solution)/shard_map/attention_grads/pallas_call | solution.py:285
  74.6 0.0 copy-start.1
  74.6 0.0 copy-start
  74.6 3.6 %copy.13 = bf16[1,640,2048]{2,1,0:T(8,128)(2,1)} copy(bf16[1,640,2048]{2,1,0:T(8,128)(2,1)} %get-tuple-element.6) | data formatting | bytes 5242880
  78.2 0.0 copy-done.1
  78.2 0.6 copy.14
  78.9 0.0 copy-done
  78.9 0.6 copy.15
Async XLA Ops:
  74.6 3.6 %copy-start.1 = (f32[1,8,2048]{2,1,0:T(8,128)S(1)}, f32[1,8,2048]{2,1,0:T(8,128)}, u32[]{:S(2)}) copy-start(f32[1,8,2048]{2,1,0:T(8,128)} %get-tuple-element.7) | copy-start | bytes 196612
  74.6 4.2 %copy-start = (f32[1,8,2048]{2,1,0:T(8,128)S(1)}, f32[1,8,2048]{2,1,0:T(8,128)}, u32[]{:S(2)}) copy-start(f32[1,8,2048]{2,1,0:T(8,128)} %get-tuple-element.8) | copy-start | bytes 196612

commit v2 on v1

v2 whole, which is shorter than its diff:
```python
import functools
import math
from typing import NamedTuple, Any

import jax
import jax.numpy as jnp
from jax import lax
from jax.experimental import pallas as pl
from jax.experimental.pallas import tpu as pltpu
from jax.sharding import PartitionSpec as P

MESH = pl.DeviceIdType.MESH
F32, BF16 = jnp.float32, jnp.bfloat16
HEAD = 128
LATENTS = 64
NX, NLO, NZ = 4, 2, 8
GROUP = NLO * NZ
PAIR, SECOND, THIRD = 2, 2, 4
PAIRED = (1, 3, 5)
LAST_SECOND, LAST_THIRD = (9, 10), (11, 11)


class Unit(NamedTuple):
    chunk: Any
    cols: Any
    sem: Any
    whole: bool


def product(a, b, ca, cb):
    return lax.dot_general(a, b, (((ca,), (cb,)), ((), ())), preferred_element_type=F32)


def kernel(
    chunks, per, q_hbm, k_hbm, v_hbm, g_hbm, gate, order, seen_hbm, dq_hbm, kg_hbm, vg_hbm,
    q_s, g_s, seen_s, stage_s, kv_s, dq_s, may_s, part_s, pair_s, a_s, b_s, bc_s, zs_s, rz_s, kg_s, vg_s,
    own_sem, round_sem, cross_tx, cross_rx, mate_tx, mate_rx, relay_tx, relay_rx,
    pair_tx, pair_rx, first_tx, a_rx, b_tx, bc_rx, z_tx, z_rx, dq_sem, grad_sem,
):
    img, txt = lax.axis_index("img"), lax.axis_index("txt")
    hi, core = img // 2, lax.rem(img, 2)
    x, lo, z = txt // GROUP, lax.rem(txt // NZ, NLO), lax.rem(txt, NZ)
    slot = lax.rem(txt, GROUP)
    zq, zp = z // 2, lax.rem(z, 2)
    mine = zp * (GROUP // 2) + lo * (NZ // 2) + zq
    tokens, width = q_s.shape
    block = k_hbm.shape[1]
    half = block // 2
    keys = 4 * block
    images = keys // LATENTS
    cw = per * HEAD
    heads = chunks * per
    part = keys // (2 * NX)
    scale = 1.0 / math.sqrt(HEAD)
    scale2 = scale * math.log2(math.e)

    mate = (hi * 2 + 1 - core, txt)
    flipped = txt + (1 - 2 * lo) * NZ
    cross = [((1 - hi) * 2 + c, flipped) for c in range(2)]
    relay = (img, flipped)
    xp, xm, xo = lax.rem(x + 1, NX), lax.rem(x + NX - 1, NX), lax.rem(x + 2, NX)
    up, down = (img, xp * GROUP + slot), (img, xm * GROUP + slot)

    before, after = (img, txt - z + lax.rem(z + NZ - 1, NZ)), (img, txt - z + lax.rem(z + 1, NZ))

    def at_place(g):
        other = lax.rem(g // (NZ // 2), NLO) * NZ + lax.rem(g, NZ // 2) * 2 + g // (GROUP // 2)
        return (img, x * GROUP + other)

    def local(src, dst, sem):
        return pltpu.make_async_copy(src, dst, sem)

    def remote(src, dst, tx, rx, to):
        return pltpu.make_async_remote_copy(
            src_ref=src, dst_ref=dst, send_sem=tx, recv_sem=rx, device_id=to, device_id_type=MESH
        )

    def columns(c, base=0):
        return pl.ds(pl.multiple_of(base + c * cw, HEAD), cw)

    def rows(start, size):
        return pl.ds(pl.multiple_of(start, 16), size)

    barrier = pltpu.get_barrier_semaphore()
    near = [mate, *cross, relay, up, down, before, after]
    for to in near:
        pl.semaphore_signal(barrier, inc=1, device_id=to, device_id_type=MESH)
    own_columns = pl.ds(pl.multiple_of(img * width, HEAD), width)
    staged = [
        local(k_hbm.at[0], stage_s.at[0], own_sem.at[0]),
        local(v_hbm.at[0], stage_s.at[1], own_sem.at[1]),
    ]
    loads = [
        local(k_hbm.at[0, :, own_columns], kv_s.at[0, img], own_sem.at[2]),
        local(v_hbm.at[0, :, own_columns], kv_s.at[1, img], own_sem.at[3]),
        local(seen_hbm, seen_s, own_sem.at[4]),
        local(q_hbm.at[0], q_s, own_sem.at[5]),
        local(g_hbm.at[0], g_s, own_sem.at[6]),
    ]
    for copy in staged + loads:
        copy.start()
    for copy in staged:
        copy.wait()
    pl.semaphore_wait(barrier, len(near))

    def tell(r):
        pl.semaphore_signal(round_sem.at[r, 0], inc=1, device_id=after, device_id_type=MESH)
        pl.semaphore_signal(round_sem.at[r, 1], inc=1, device_id=before, device_id_type=MESH)

    def hear(r):
        pl.semaphore_wait(round_sem.at[r, 0], 1)
        pl.semaphore_wait(round_sem.at[r, 1], 1)

    tell(0)

    def one_head(h, base=0):
        return pl.ds(pl.multiple_of(base + h * HEAD, HEAD), HEAD)

    def cross_piece(h):
        return kv_s.at[:, pl.ds(2 * (1 - hi), 2), rows(lo * half, half), one_head(h)]

    def relay_piece(h):
        return kv_s.at[:, pl.ds(2 * (1 - hi), 2), rows((1 - lo) * half, half), one_head(h)]

    def mate_piece(h):
        return kv_s.at[:, hi * 2 + 1 - core, :, one_head(h)]

    def cross_send(h, to):
        sent = rows((1 - lo) * half, half)
        return remote(
            stage_s.at[:, sent, one_head(h, to[0] * width)], kv_s.at[:, img, sent, one_head(h)],
            cross_tx.at[h], cross_rx.at[h], to,
        )

    def mate_send(h):
        return remote(
            stage_s.at[:, :, one_head(h, mate[0] * width)], kv_s.at[:, img, :, one_head(h)],
            mate_tx.at[h], mate_rx.at[h], mate,
        )

    def send_latents(h, carry):
        for to in cross:
            cross_send(h, to).start()
        mate_send(h).start()
        return carry

    lax.fori_loop(0, heads, send_latents, 0)
    hear(0)
    tell(1)
    for copy in loads:
        copy.wait()
    may_s[...] = jnp.concatenate(
        [jnp.where(order[0, b] < seen_s[...].reshape(1, tokens), 1.0, 0.0) for b in range(images)],
        axis=0,
    )

    def pass_on(h):
        piece = cross_piece(h)
        remote(piece, piece, cross_tx.at[h], cross_rx.at[h], relay).wait_recv()
        remote(piece, piece, relay_tx.at[h], relay_rx.at[h], relay).start()

    def latents_ready(h):
        piece = mate_piece(h)
        remote(piece, piece, mate_tx.at[h], mate_rx.at[h], mate).wait_recv()

        piece = relay_piece(h)
        remote(piece, piece, relay_tx.at[h], relay_rx.at[h], relay).wait_recv()

    def keep(c, a, at, value):
        by_parity = value.reshape(keys // 16, 2, 8, HEAD)
        for p in range(2):
            rows_p = by_parity[:, p].reshape(NX, part, HEAD)
            part_s[c, p, a, :, :, at] = rows_p.astype(BF16)

    def head(c, j):
        h = c * per + j
        cols = pl.ds(pl.multiple_of(h * HEAD, HEAD), HEAD)
        k = kv_s[0, :, :, cols].reshape(keys, HEAD)
        v = kv_s[1, :, :, cols].reshape(keys, HEAD)
        q = q_s[:, cols]
        factor = jnp.tanh(jnp.full((8, HEAD), gate[0, h], F32))[0:1]
        gated = (g_s[:, cols].astype(F32) * factor).astype(BF16)
        may = may_s[...] > 0
        scores = product(k, q, 1, 1).reshape(images, LATENTS, tokens)
        top = jnp.where(may, jnp.max(scores, axis=1), -1e30)
        top = jnp.max(top, axis=0, keepdims=True)
        off = jnp.where(may, top, 1e30)
        exponent = jnp.exp2((scores - off[:, None, :]) * scale2).reshape(keys, tokens)
        weights = exponent * (1.0 / jnp.sum(exponent, axis=0, keepdims=True))
        weight_grad = product(v, gated, 1, 1)
        delta = jnp.sum(weights * weight_grad, axis=0, keepdims=True)
        score_half = (weights * (weight_grad - delta)).astype(BF16)
        weight_half = weights.astype(BF16)
        at = pl.ds(j * HEAD, HEAD)
        keep(c, 1, at, product(weight_half, gated, 1, 0))
        keep(c, 0, at, product(score_half, q, 1, 0) * scale)
        dq_s[:, cols] = (product(score_half, k, 0, 0) * scale).astype(BF16)

    def dq_copy(c):
        return local(dq_s.at[:, columns(c)], dq_hbm.at[0, :, columns(c)], dq_sem.at[c])

    def pair_of(c):
        odd = lax.rem(c // 2, 2)
        return jnp.where(zp == odd, 1, -1)

    def pair_send(u):
        c = u.chunk
        to = (img, txt - z + lax.rem(z + NZ + pair_of(c), NZ))
        return remote(part_s.at[c, 1 - zp], pair_s.at[c], pair_tx.at[c], pair_rx.at[c], to)

    def pair_sum(u):
        c = u.chunk
        pair_send(u).wait_recv()
        for a in range(2):
            for i in range(NX):
                both = part_s[c, zp, a, i].astype(F32) + pair_s[c, a, i].astype(F32)
                part_s[c, zp, a, i] = both.astype(BF16)

    def parities(u):
        return pl.ds(0, 2) if u.whole else pl.ds(0, 1)

    def slab_of(u, a, i):
        return part_s.at[u.chunk, pl.ds(0, 2) if u.whole else pl.ds(zp, 1), a, i, :, u.cols]

    def a_of(u, a):
        return a_s.at[u.chunk, a, parities(u), :, u.cols]

    def b_of(u, a):
        return b_s.at[u.chunk, a, parities(u), :, u.cols]

    def bc_of(u, hop, a):
        return bc_s.at[u.chunk, hop, a, parities(u), :, u.cols]

    both_arrays = pl.ds(0, 2)

    def first_sends(u):
        tx, rx_a, rx_c = first_tx.at[u.sem], a_rx.at[u.sem], bc_rx.at[u.sem]
        return [
            remote(slab_of(u, 0, xo), a_of(u, 0), tx, rx_a, down),
            remote(slab_of(u, 1, xo), a_of(u, 1), tx, rx_a, up),
            remote(slab_of(u, 0, xp), bc_of(u, 1, 0), tx, rx_c, up),
            remote(slab_of(u, 1, xm), bc_of(u, 1, 1), tx, rx_c, down),
        ]

    def second_sends(u):
        return [
            remote(b_of(u, a), bc_of(u, 0, a), b_tx.at[u.sem], bc_rx.at[u.sem], to)
            for a, to in enumerate((down, up))
        ]

    def second_hop(u):
        piece = a_of(u, both_arrays)
        remote(piece, piece, first_tx.at[u.sem], a_rx.at[u.sem], down).wait_recv()
        for a, i in enumerate((xm, xp)):
            for p in range(2 if u.whole else 1):
                own = part_s[u.chunk, p if u.whole else zp, a, i, :, u.cols].astype(F32)
                total = a_s[u.chunk, a, p, :, u.cols].astype(F32) + own
                b_s[u.chunk, a, p, :, u.cols] = total.astype(BF16)

    def x_sum(u):
        piece = bc_of(u, pl.ds(0, 2), both_arrays)
        remote(piece, piece, b_tx.at[u.sem], bc_rx.at[u.sem], down).wait_recv()
        c = u.chunk
        for p in range(2 if u.whole else 1):
            parity = p if u.whole else zp
            both = [
                (
                    part_s[c, parity, a, x, :, u.cols].astype(F32)
                    + bc_s[c, 0, a, p, :, u.cols].astype(F32)
                    + bc_s[c, 1, a, p, :, u.cols].astype(F32)
                ).reshape(GROUP // 2, 8, u.cols.size)
                for a in range(2)
            ]
            places = pl.ds(parity * (GROUP // 2), GROUP // 2)
            zs_s[c, places, :, u.cols] = jnp.concatenate(both, axis=1).astype(BF16)
        rz_s[c, mine, :, u.cols] = zs_s[c, mine, :, u.cols]

    def spread(u):
        size = GROUP if u.whole else GROUP // 2

        def one(j, carry):
            if u.whole:
                g = lax.rem(mine + j, GROUP)
            else:
                g = zp * size + lax.rem(mine + j, size)
            remote(
                zs_s.at[u.chunk, g, :, u.cols], rz_s.at[u.chunk, mine, :, u.cols],
                z_tx.at[u.sem], z_rx.at[u.sem], at_place(g),
            ).start()
            return carry

        lax.fori_loop(1, size, one, 0)

    def others(ref, u):
        return ref.at[u.chunk, pl.ds(0, (GROUP if u.whole else GROUP // 2) - 1), :, u.cols]

    def finish(u):
        piece = others(rz_s, u)
        remote(piece, piece, z_tx.at[u.sem], z_rx.at[u.sem], relay).wait_recv()
        places = pl.ds(0, GROUP) if u.whole else pl.ds(zp * (GROUP // 2), GROUP // 2)
        total = jnp.sum(rz_s[u.chunk, places, :, u.cols].astype(F32), axis=0)
        at = grad_columns(u)
        kg_s[:, at] = total[:8]
        vg_s[:, at] = total[8:]
        for copy in grad_copies(at, u.sem):
            copy.start()

    def grad_columns(u):
        if isinstance(u.chunk, int):
            return pl.ds(u.chunk * cw + u.cols.start, u.cols.size)
        return columns(u.chunk)

    def grad_copies(at, sem):
        return [
            local(kg_s.at[:, at], kg_hbm.at[0, :, at], grad_sem.at[sem, 0]),
            local(vg_s.at[:, at], vg_hbm.at[0, :, at], grad_sem.at[sem, 1]),
        ]

    def start(copies):
        for copy in copies:
            copy.start()

    def after_compute(u):
        if u.whole:
            start(first_sends(u))
        else:
            pair_send(u).start()

    def first_stage(u):
        pair_sum(u)
        start(first_sends(u))

    def second_stage(u):
        second_hop(u)
        start(second_sends(u))

    def third_stage(u):
        x_sum(u)
        spread(u)

    def unit(c, whole):
        return Unit(c, pl.ds(0, cw), c, whole)

    last = chunks - 1
    ends = [Unit(last, pl.ds(j * HEAD, HEAD), last + j, True) for j in range(per)]

    def paired(c):
        return functools.reduce(lambda t, d: t | (c == d), PAIRED, c < 0)

    def each(c, act, forms=(True, False)):
        for whole in forms:
            fits = (c >= 0) & (c < last) & (paired(c) != whole)
            pl.when(fits)(functools.partial(act, unit(c, whole)))

    def compute(h, c, j):
        @pl.when(h + 2 < heads)
        def _():
            pass_on(h + 2)

        latents_ready(h)
        head(c, j)

    hear(1)
    tell(2)
    pass_on(0)
    hear(2)
    tell(3)
    pass_on(1)

    def step(s, carry):
        def one(j, inner):
            compute(s * per + j, s, j)
            return inner

        lax.fori_loop(0, per, one, 0)
        dq_copy(s).start()
        each(s, after_compute)
        pl.when(s == 0)(lambda: hear(3))
        each(s - PAIR, first_stage, (False,))
        each(s - SECOND, second_stage, (True,))
        each(s - PAIR - SECOND, second_stage, (False,))
        each(s - THIRD, third_stage, (True,))
        each(s - PAIR - THIRD, third_stage, (False,))
        return carry

    lax.fori_loop(0, last, step, 0)
    for j, u in enumerate(ends):
        compute(last * per + j, last, j)
        after_compute(u)

    dq_copy(last).start()

    due = {}
    for c in range(last):
        late = PAIR if c in PAIRED else 0
        for at, act in ((0, first_stage), (SECOND, second_stage), (THIRD, third_stage)):
            if c + late + at >= last and (at or late):
                due.setdefault(c + late + at, []).append((act, unit(c, c not in PAIRED)))
    for u, second, third in zip(ends, LAST_SECOND, LAST_THIRD):
        due.setdefault(second, []).append((second_stage, u))
        due.setdefault(third, []).append((third_stage, u))
    def settle_head(h, carry):
        piece = cross_piece(h)
        remote(piece, piece, cross_tx.at[h], cross_rx.at[h], relay).wait_send()
        remote(piece, piece, relay_tx.at[h], relay_rx.at[h], relay).wait_send()
        mate_send(h).wait_send()
        return carry

    def settle_unit(u):
        if not u.whole:
            pair_send(u).wait_send()
        piece = bc_of(u, pl.ds(0, 2), both_arrays)
        remote(piece, piece, first_tx.at[u.sem], bc_rx.at[u.sem], down).wait_send()
        piece = b_of(u, both_arrays)
        remote(piece, piece, b_tx.at[u.sem], bc_rx.at[u.sem], down).wait_send()
        piece = others(zs_s, u)
        remote(piece, piece, z_tx.at[u.sem], z_rx.at[u.sem], relay).wait_send()

    def settle_grads(u):
        for copy in grad_copies(grad_columns(u), u.sem):
            copy.wait()

    def settle(c, carry):
        dq_copy(c).wait()
        each(c, settle_unit)
        return carry

    def settle_all_grads(c, carry):
        each(c, settle_grads)
        return carry

    for s in sorted(due):
        for act, u in due[s]:
            act(u)
        if s == last:
            lax.fori_loop(0, heads, settle_head, 0)

    def end(c, carry):
        each(c, finish)
        return carry

    lax.fori_loop(0, last - 1, settle, 0)
    lax.fori_loop(0, last, end, 0)
    for u in ends:
        finish(u)
    lax.fori_loop(last - 1, chunks, settle, 0)
    lax.fori_loop(0, last, settle_all_grads, 0)
    for u in ends:
        settle_unit(u)
        settle_grads(u)


def hand_on(dq_in, kg_in, vg_in, dq_out, kg_out, vg_out, dq_s, grad_s, sem):
    steps = dq_s.shape[0]
    rows = dq_s.shape[1]
    pairs = [
        (dq_in.at[0, pl.ds(i * rows, rows)], dq_s.at[i], dq_out.at[0, pl.ds(i * rows, rows)])
        for i in range(steps)
    ]
    pairs += [(kg_in.at[0], grad_s.at[0], kg_out.at[0]), (vg_in.at[0], grad_s.at[1], vg_out.at[0])]
    loads = [pltpu.make_async_copy(a, b, sem.at[0, i]) for i, (a, b, _) in enumerate(pairs)]
    stores = [pltpu.make_async_copy(b, c, sem.at[1, i]) for i, (_, b, c) in enumerate(pairs)]
    for copy in loads:
        copy.start()
    for load, store in zip(loads, stores):
        load.wait()
        store.start()
    for copy in stores:
        copy.wait()


def shards(queries, visual_keys, visual_values, out_grad, gate_value, image_order, image_seen):
    _, tokens, width = queries.shape
    block = visual_keys.shape[1]
    keys = 4 * block
    heads = width // HEAD
    per = 2
    chunks = heads // per
    cw = per * HEAD
    part = keys // (2 * NX)
    mine = keys // (NX * GROUP)
    hbm = pl.BlockSpec(memory_space=pl.ANY)
    smem = pl.BlockSpec(memory_space=pltpu.SMEM)
    dma = pltpu.SemaphoreType.DMA
    outs = tuple(
        pl.pallas_call(
            functools.partial(kernel, chunks, per),
            out_shape=(
                jax.ShapeDtypeStruct((1, tokens, width), BF16),
                jax.ShapeDtypeStruct((1, mine, width), F32),
                jax.ShapeDtypeStruct((1, mine, width), F32),
            ),
            in_specs=[hbm, hbm, hbm, hbm, smem, smem, hbm],
            out_specs=(hbm, hbm, hbm),
            scratch_shapes=[
                pltpu.VMEM((tokens, width), BF16),
                pltpu.VMEM((tokens, width), BF16),
                pltpu.VMEM((tokens,), jnp.int32),
                pltpu.VMEM((2, block, 4 * width), BF16),
                pltpu.VMEM((2, 4, block, width), BF16),
                pltpu.VMEM((tokens, width), BF16),
                pltpu.VMEM((keys // LATENTS, tokens), F32),
                pltpu.VMEM((chunks, 2, 2, NX, part, cw), BF16),
                pltpu.VMEM((chunks, 2, NX, part, cw), BF16),
                pltpu.VMEM((chunks, 2, 2, part, cw), BF16),
                pltpu.VMEM((chunks, 2, 2, part, cw), BF16),
                pltpu.VMEM((chunks, 2, 2, 2, part, cw), BF16),
                pltpu.VMEM((chunks, GROUP, 2 * mine, cw), BF16),
                pltpu.VMEM((chunks, GROUP, 2 * mine, cw), BF16),
                pltpu.VMEM((mine, width), F32),
                pltpu.VMEM((mine, width), F32),
                dma((7,)),
                pltpu.SemaphoreType.REGULAR((4, 2)),
            ]
            + [dma((heads,))] * 6
            + [dma((chunks + 1,))] * 9
            + [dma((chunks + 1, 2))],
            compiler_params=pltpu.CompilerParams(
                collective_id=0, has_side_effects=True, vmem_limit_bytes=60 * 2**20
            ),
            name="attention_grads",
        )(
            queries, visual_keys, visual_values, out_grad, gate_value, image_order,
            image_seen,
        )
    )
    steps = 5
    return tuple(
        pl.pallas_call(
            hand_on,
            out_shape=tuple(jax.ShapeDtypeStruct(o.shape, o.dtype) for o in outs),
            in_specs=[hbm] * 3,
            out_specs=(hbm,) * 3,
            scratch_shapes=[
                pltpu.VMEM((steps, tokens // steps, width), BF16),
                pltpu.VMEM((2, mine, width), F32),
                dma((2, steps + 2)),
            ],
            compiler_params=pltpu.CompilerParams(vmem_limit_bytes=60 * 2**20),
            name="hand_on",
        )(*outs)
    )


def solution(mesh):
    placed = (
        P(None, "txt", "img"),
        P(None, "img", None),
        P(None, "img", None),
        P(None, "txt", "img"),
        P(None, "img"),
        P(),
        P("txt"),
    )
    return jax.shard_map(
        shards,
        mesh=mesh,
        in_specs=placed,
        out_specs=(P(None, "txt", "img"), P(None, "txt", "img"), P(None, "txt", "img")),
        check_vma=False,
    )
```

time: 79.7 us -> 69.8 us (0.88)
  local copies, waits for them, and re-layouts: 6.13 us -> 0 us
  Pallas kernels: 72.7 us -> 69 us
    pallas_call x1, Pallas kernels: 72.7 us -> 66.3 us  [shards(): pl.pallas_call(functools.partial(kernel, chunks, per), out_shape=(jax.Sha...]
    unnamed x7 -> x0, local copies, waits for them, and re-layouts: 4.86 us -> none
    pallas_call x0 -> x1, Pallas kernels: none -> 2.68 us  [shards(): pl.pallas_call(hand_on, out_shape=tuple((jax.ShapeDtypeStruct(o.shape, o....]
    reshape x1 -> x0, local copies, waits for them, and re-layouts: 1.27 us -> none  [shards(): image_seen.reshape(1, tokens)]
where the time goes in v2:
time: 69.8 us; the launch traced here: 69.7 us
  Pallas kernels  69 us (99%)
    pallas_call x1, Pallas kernels, shards(): pl.pallas_call(functools.partial(kernel, chunks, per), out_shape=(jax.Sha...  66.3 us
    pallas_call x1, Pallas kernels, shards(): pl.pallas_call(hand_on, out_shape=tuple((jax.ShapeDtypeStruct(o.shape, o....  2.68 us

profile of v2, /device:TPU:2, one launch (start us, length us, event | category | flops | bytes accessed | tf_op | source)
XLA Modules:
  0.0 69.7 jit_solution(8780421520458905558)
XLA Ops:
  0.6 66.3 %attention_grads.1 = (bf16[1,640,2048]{2,1,0:T(8,128)(2,1)}, f32[1,8,2048]{2,1,0:T(8,128)}, f32[1,8,2048]{2,1,0:T(8,128)}) custom-call(bf16[1,640,2048]{2,1,0:T(8,128)(2,1)} %q_hbm.1, bf16[1,128,8192]{2,1,0:T(8,128)(2,1)} %k_hbm.1, bf16[1,128,8192]{2,1,0:T(8,128)(2,1)} %v_hbm.1, bf16[1,640,2048]{2,1,0:T(8,128)(2,1)} %g_hbm.1, f32[1,16]{1,0:T(1,128)} %gate.1, ...), custom_call_target="tpu_custom_call" | custom-call | tf_op jit(solution)/shard_map/attention_grads/pallas_call | solution.py:486
  67.0 2.7 %hand_on.1 = (bf16[1,640,2048]{2,1,0:T(8,128)(2,1)}, f32[1,8,2048]{2,1,0:T(8,128)}, f32[1,8,2048]{2,1,0:T(8,128)}) custom-call(bf16[1,640,2048]{2,1,0:T(8,128)(2,1)} %get-tuple-element.6.dq_in, f32[1,8,2048]{2,1,0:T(8,128)} %get-tuple-element.7.kg_in, f32[1,8,2048]{2,1,0:T(8,128)} %get-tuple-element.8.vg_in), custom_call_target="tpu_custom_call" | custom-call | tf_op jit(solution)/shard_map/hand_on/pallas_call | solution.py:529

commit v3 on v2

--- a/solution.py
+++ b/solution.py
@@ -16,7 +16,7 @@
 NX, NLO, NZ = 4, 2, 8
 GROUP = NLO * NZ
 PAIR, SECOND, THIRD = 2, 2, 4
-PAIRED = (1, 3, 5)
+PAIRED = (1, 5)
 LAST_SECOND, LAST_THIRD = (9, 10), (11, 11)
 
 

time: 69.8 us -> 69 us (0.989)
  Pallas kernels: 69 us -> 68.2 us
    pallas_call x1, Pallas kernels: 66.3 us -> 65.5 us  [shards(): pl.pallas_call(functools.partial(kernel, chunks, per), out_shape=(jax.Sha...]
where the time goes in v3:
time: 69 us; the launch traced here: 68.8 us
  Pallas kernels  68.2 us (99%)
    pallas_call x1, Pallas kernels, shards(): pl.pallas_call(functools.partial(kernel, chunks, per), out_shape=(jax.Sha...  65.5 us
    pallas_call x1, Pallas kernels, shards(): pl.pallas_call(hand_on, out_shape=tuple((jax.ShapeDtypeStruct(o.shape, o....  2.68 us

profile of v3, /device:TPU:2, one launch (start us, length us, event | category | flops | bytes accessed | tf_op | source)
XLA Modules:
  0.0 68.8 jit_solution(13094670641999524115)
XLA Ops:
  0.6 65.5 %attention_grads.1 = (bf16[1,640,2048]{2,1,0:T(8,128)(2,1)}, f32[1,8,2048]{2,1,0:T(8,128)}, f32[1,8,2048]{2,1,0:T(8,128)}) custom-call(bf16[1,640,2048]{2,1,0:T(8,128)(2,1)} %q_hbm.1, bf16[1,128,8192]{2,1,0:T(8,128)(2,1)} %k_hbm.1, bf16[1,128,8192]{2,1,0:T(8,128)(2,1)} %v_hbm.1, bf16[1,640,2048]{2,1,0:T(8,128)(2,1)} %g_hbm.1, f32[1,16]{1,0:T(1,128)} %gate.1, ...), custom_call_target="tpu_custom_call" | custom-call | tf_op jit(solution)/shard_map/attention_grads/pallas_call | solution.py:486
  66.1 2.7 %hand_on.1 = (bf16[1,640,2048]{2,1,0:T(8,128)(2,1)}, f32[1,8,2048]{2,1,0:T(8,128)}, f32[1,8,2048]{2,1,0:T(8,128)}) custom-call(bf16[1,640,2048]{2,1,0:T(8,128)(2,1)} %get-tuple-element.6.dq_in, f32[1,8,2048]{2,1,0:T(8,128)} %get-tuple-element.7.kg_in, f32[1,8,2048]{2,1,0:T(8,128)} %get-tuple-element.8.vg_in), custom_call_target="tpu_custom_call" | custom-call | tf_op jit(solution)/shard_map/hand_on/pallas_call | solution.py:529

commit v4 on v3

--- a/solution.py
+++ b/solution.py
@@ -278,18 +278,20 @@
     def spread(u):
         size = GROUP if u.whole else GROUP // 2
 
-        def one(j, carry):
-            if u.whole:
-                g = lax.rem(mine + j, GROUP)
-            else:
-                g = zp * size + lax.rem(mine + j, size)
+        stride = 1 if u.whole else 2
+
+        def one(t, carry):
+            m = t // 2
+            dz = NZ // 2 + stride * ((m + 1) // 2) * (1 - 2 * lax.rem(m, 2))
+            y, zz = lax.rem(lo + 1 + t, NLO), lax.rem(z + dz, NZ)
+            g = lax.rem(zz, 2) * (GROUP // 2) + y * (NZ // 2) + zz // 2
             remote(
                 zs_s.at[u.chunk, g, :, u.cols], rz_s.at[u.chunk, mine, :, u.cols],
                 z_tx.at[u.sem], z_rx.at[u.sem], at_place(g),
             ).start()
             return carry
 
-        lax.fori_loop(1, size, one, 0)
+        lax.fori_loop(0, size - 1, one, 0)
 
     def others(ref, u):
         return ref.at[u.chunk, pl.ds(0, (GROUP if u.whole else GROUP // 2) - 1), :, u.cols]

time: 69 us -> 69.5 us (level)
  no operation moved by 1% of the time
where the time goes in v4:
time: 69.5 us; the launch traced here: 68.7 us
  Pallas kernels  68.1 us (98%)
    pallas_call x1, Pallas kernels, shards(): pl.pallas_call(functools.partial(kernel, chunks, per), out_shape=(jax.Sha...  65.4 us
    pallas_call x1, Pallas kernels, shards(): pl.pallas_call(hand_on, out_shape=tuple((jax.ShapeDtypeStruct(o.shape, o....  2.68 us

profile of v4, /device:TPU:2, one launch (start us, length us, event | category | flops | bytes accessed | tf_op | source)
XLA Modules:
  0.0 68.7 jit_solution(15977435810547530075)
XLA Ops:
  0.6 65.4 %attention_grads.1 = (bf16[1,640,2048]{2,1,0:T(8,128)(2,1)}, f32[1,8,2048]{2,1,0:T(8,128)}, f32[1,8,2048]{2,1,0:T(8,128)}) custom-call(bf16[1,640,2048]{2,1,0:T(8,128)(2,1)} %q_hbm.1, bf16[1,128,8192]{2,1,0:T(8,128)(2,1)} %k_hbm.1, bf16[1,128,8192]{2,1,0:T(8,128)(2,1)} %v_hbm.1, bf16[1,640,2048]{2,1,0:T(8,128)(2,1)} %g_hbm.1, f32[1,16]{1,0:T(1,128)} %gate.1, ...), custom_call_target="tpu_custom_call" | custom-call | tf_op jit(solution)/shard_map/attention_grads/pallas_call | solution.py:488
  66.0 2.7 %hand_on.1 = (bf16[1,640,2048]{2,1,0:T(8,128)(2,1)}, f32[1,8,2048]{2,1,0:T(8,128)}, f32[1,8,2048]{2,1,0:T(8,128)}) custom-call(bf16[1,640,2048]{2,1,0:T(8,128)(2,1)} %get-tuple-element.6.dq_in, f32[1,8,2048]{2,1,0:T(8,128)} %get-tuple-element.7.kg_in, f32[1,8,2048]{2,1,0:T(8,128)} %get-tuple-element.8.vg_in), custom_call_target="tpu_custom_call" | custom-call | tf_op jit(solution)/shard_map/hand_on/pallas_call | solution.py:531
